TPU v7x, 32 devices: a whole 2x2x4 slice. The times are simulated.
32 devices in a mesh: grp: 2 (over x), seq: 8 (over z, y), head: 2 (over core).
Axes of the slice: x: 2, y: 2, z: 4, core: 2. Of those that a mesh axis runs over, the one named last changes fastest.
Arguments:
- inputs: float32 [4096, 4096], P(('grp', 'seq'), 'head'), parts along dimension 0, may hold values from -6 to 6
- rates: float32 [64, 4096], P('head', ('grp', 'seq')), parts along dimension 1, may hold values from 0.5 to 2
- decay_rate: float32 [64], P('head'), may hold values from 0.00048828125 to 0.03
- skip: float32 [64], P('head'), may hold values from 0.5 to 1.5
- keys_b: float32 [4096, 128], P(('grp', 'seq')), parts along dimension 0, may hold values from -0.5 to 0.5
- keys_c: float32 [4096, 128], P(('grp', 'seq')), parts along dimension 0, may hold values from -0.5 to 0.5
- grad_out: float32 [4096, 4096], P(('grp', 'seq'), 'head'), parts along dimension 0, may hold values from -6 to 6
Outputs:
- output: float32 [4096, 4096], P(('grp', 'seq'), 'head'), parts along dimension 0
- grad_inputs: float32 [4096, 4096], P(('grp', 'seq'), 'head'), parts along dimension 0
- input_key_gradient: float32 [4096, 128], P(('grp', 'seq')), parts along dimension 0
- output_key_gradient: float32 [4096, 128], P(('grp', 'seq')), parts along dimension 0
There are 2 independent parts, one for each index of `grp`. A program takes and returns all parts, laid end to end along the dimension named above; an argument that names none is the same for every part. Nothing has to cross between parts.
All inputs are finite; a program needn't handle non-finite values.
Results may differ from a plain program's by a relative error of at most 0.00016.
Values sent between devices are 32-bit elements; how exact they have to be, the bound alone decides.
A program may use at most 192 MiB of HBM per device.

v0:
```python
import jax
import jax.numpy as jnp
from jax import lax
from jax.sharding import PartitionSpec as P

Q = 128


HIGH = lax.Precision.HIGHEST


def carried_in(array, axis, combine, identity, reverse):
    size, mine = (lax.axis_size(axis), lax.axis_index(axis))
    everything = jax.tree.map(lambda part: lax.all_gather(part, axis), array)
    start = jax.tree.map(
        lambda part, zero: jnp.broadcast_to(jnp.asarray(zero, part.dtype), part.shape),
        array,
        identity,
    )

    def turn(k, before):
        at = size - 1 - k if reverse else k
        reached = at > mine if reverse else at < mine
        new = combine(before, jax.tree.map(lambda part: part[at], everything))
        return jax.tree.map(lambda a, b: jnp.where(reached, a, b), new, before)

    return lax.fori_loop(0, size, turn, start)


def mixed_output(form, left, right):
    return jnp.einsum(form, left, right, precision=HIGH)


def decays(rates, decay_rate, block):
    heads, length = rates.shape
    count = length // block
    logs = -(decay_rate[:, None] * rates).reshape(heads, count, block)
    inner = jnp.cumsum(logs, axis=2)
    ends = inner[:, :, -1]
    starts = jnp.cumsum(ends, axis=1) - ends
    total = jnp.sum(ends, axis=1)
    rows = lax.broadcasted_iota(jnp.int32, (block, block), 0)
    cols = lax.broadcasted_iota(jnp.int32, (block, block), 1)
    gap = inner[:, :, :, None] - inner[:, :, None, :]
    within = jnp.where(rows >= cols, jnp.exp(jnp.where(rows >= cols, gap, 0.0)), 0.0)
    upper = lax.broadcasted_iota(jnp.int32, (count, count), 0)
    lower = lax.broadcasted_iota(jnp.int32, (count, count), 1)
    span = starts[:, :, None] - starts[:, None, :] - ends[:, None, :]
    across = jnp.where(upper > lower, jnp.exp(jnp.where(upper > lower, span, 0.0)), 0.0)
    return (inner, ends, starts, total, within, across)


def layer(inputs, rates, decay_rate, skip, keys_b, keys_c, grads, incoming, outgoing, block):
    length, heads, width = inputs.shape
    count = length // block
    state_size = keys_b.shape[1]
    inner, ends, starts, total, within, across = decays(rates, decay_rate, block)
    input_rows = inputs.reshape(count, block, heads, width)
    dys = grads.reshape(count, block, heads, width)
    input_key_rows = keys_b.reshape(count, block, state_size)
    output_key_rows = keys_c.reshape(count, block, state_size)
    steps = rates.reshape(heads, count, block)
    scores = mixed_output("ctn,csn->cts", output_key_rows, input_key_rows)
    weighted = within * scores[None]
    intra = mixed_output("hcts,cshp->cthp", weighted * steps[:, :, None, :], input_rows)
    tail_segment = jnp.transpose(jnp.exp(ends[:, :, None] - inner) * steps, (1, 2, 0))[..., None]
    growth = jnp.transpose(jnp.exp(inner), (1, 2, 0))[..., None]
    stretch_states = mixed_output("cshp,csn->hcpn", input_rows * tail_segment, input_key_rows)
    entering_state = mixed_output("hck,hkpn->hcpn", across, stretch_states)
    closing = jnp.exp(total[:, None] - starts - ends)
    final = mixed_output("hc,hcpn->hpn", closing, stretch_states)
    seg_decay = jnp.exp(total)
    first_state = incoming(seg_decay, final)
    entering_state = entering_state + jnp.exp(starts)[:, :, None, None] * first_state[:, None]
    output = (
        intra
        + mixed_output("hcpn,ctn->cthp", entering_state, output_key_rows) * growth
        + skip[None, None, :, None] * input_rows
    )
    scaled_output_gradient = dys * growth
    pushed = mixed_output("cshp,csn->hcpn", scaled_output_gradient, output_key_rows)
    later = mixed_output("hkc,hkpn->hcpn", across, pushed)
    opening = mixed_output("hc,hcpn->hpn", jnp.exp(starts), pushed)
    last_adjoint = outgoing(seg_decay, opening)
    adjoint_state = later + closing[:, :, None, None] * last_adjoint[:, None]
    step_t = jnp.transpose(steps, (1, 2, 0))[..., None]
    grad_x = mixed_output("hcst,cshp->cthp", weighted, dys) * step_t
    grad_x = (
        grad_x
        + mixed_output("hcpn,ctn->cthp", adjoint_state, input_key_rows) * tail_segment
        + skip[None, None, :, None] * dys
    )
    products = jnp.einsum("cahp,cbhp->hcab", dys, input_rows, precision=HIGH)
    masked_scores = within * products * steps[:, :, None, :]
    output_key_gradient = mixed_output(
        "qsgm,smd->sgd", masked_scores, input_key_rows
    ) + mixed_output("jizk,zjky->jiy", scaled_output_gradient, entering_state)
    input_key_gradient = mixed_output(
        "megv,egs->evs", masked_scores, output_key_rows
    ) + mixed_output("jizk,zjky->jiy", input_rows * tail_segment, adjoint_state)
    return (
        output.reshape(length, heads, width),
        grad_x.reshape(length, heads, width),
        input_key_gradient.reshape(length, state_size),
        output_key_gradient.reshape(length, state_size),
    )


def join_forward(earlier, later):
    return (earlier[0] * later[0], later[0][:, None, None] * earlier[1] + later[1])


def join_backward(earlier, later):
    return (earlier[0] * later[0], later[1] + later[0][:, None, None] * earlier[1])


def body(inputs, rates, decay_rate, skip, keys_b, keys_c, grad_out):
    tokens = inputs.shape[0]
    heads = rates.shape[0]
    width = inputs.shape[1] // heads
    block = Q
    values = inputs.reshape(tokens, heads, width)
    grads = grad_out.reshape(tokens, heads, width)

    def carry_in(seg_decay, states):
        result = carried_in(
            (seg_decay, states),
            "seq",
            join_forward,
            (jnp.ones_like(seg_decay), jnp.zeros_like(states)),
            False,
        )
        return result[1]

    def carry_back(seg_decay, states):
        result = carried_in(
            (seg_decay, states),
            "seq",
            join_backward,
            (jnp.ones_like(seg_decay), jnp.zeros_like(states)),
            True,
        )
        return result[1]

    output, grad_x, term_b, term_c = layer(
        values, rates, decay_rate, skip, keys_b, keys_c, grads, carry_in, carry_back, block
    )
    input_key_gradient, output_key_gradient = lax.psum((term_b, term_c), "head")
    return (
        output.reshape(tokens, heads * width),
        grad_x.reshape(tokens, heads * width),
        input_key_gradient,
        output_key_gradient,
    )


def solution(mesh):
    in_specs = (
        P(("grp", "seq"), "head"),
        P("head", ("grp", "seq")),
        P("head"),
        P("head"),
        P(("grp", "seq"), None),
        P(("grp", "seq"), None),
        P(("grp", "seq"), "head"),
    )
    out_specs = (
        P(("grp", "seq"), "head"),
        P(("grp", "seq"), "head"),
        P(("grp", "seq"), None),
        P(("grp", "seq"), None),
    )
    return jax.shard_map(body, mesh=mesh, in_specs=in_specs, out_specs=out_specs, check_vma=False)
```

profile of v0, /device:TPU:0, one launch (start us, length us, event | category | flops | bytes accessed | tf_op | source)
XLA Modules:
  0.0 366.2 jit_solution(17702076972483568150)
XLA Ops:
  9.8 2.9 copy.86
  12.7 2.3 reshape_reshape.14
  15.1 1.9 fusion.44
  17.0 8.9 %fusion.47 = f32[32,1,64,128]{3,1,2,0:T(1,128)} fusion(f32[32,2,1,1]{1,2,3,0:T(1,128)S(1)} %copy.109, f32[32,2,64,128]{3,2,0,1:T(8,128)S(1)} %fusion.44), kind=kOutput, calls=%fused_computation.47 | convolution fusion | flops 6291456 | bytes 3145984 | tf_op jit(solution)/shard_map/hc,hcpn->hpn/dot_general | solution.py:31
  26.3 2.9 copy.71
  29.2 2.3 reshape_reshape.12
  32.2 1.9 fusion.41
  35.4 8.9 %fusion.50 = f32[32,1,64,128]{3,1,2,0:T(1,128)} fusion(f32[32,2,1,1]{1,2,3,0:T(1,128)S(1)} %copy.105, f32[32,2,64,128]{3,2,0,1:T(8,128)S(1)} %fusion.41), kind=kOutput, calls=%fused_computation.50 | convolution fusion | flops 6291456 | bytes 3145984 | tf_op jit(solution)/shard_map/hc,hcpn->hpn/dot_general | solution.py:31
  48.5 24.7 %all-reduce = f32[256]{0:T(256)S(1)} all-reduce(f32[256]{0:T(256)S(1)} %exponential_dynamic-update-slice_fusion), channel_id=2, replica_groups=mesh['grp'=2,'seq'=8,'head'=2] {'seq'}, use_global_device_ids=true, to_apply=%add | all-reduce | flops 256 | bytes 2048
  74.6 1.4 slice_subtract_fusion
  77.1 1.3 copy.82
  78.5 1.4 copy.89
  80.8 4.9 %fusion.6 = (f32[32,2,128,128]{3,2,1,0:T(8,128)}, f32[32,2,128,128]{3,2,1,0:T(8,128)}) fusion(f32[2,128,128]{2,1,0:T(8,128)S(1)} %fusion.71, f32[32,2,128]{2,1,0:T(2,128)S(1)} %copy.69, pred[128,128]{1,0:T(8,128)(4,1)S(1)} %iota_compare_fusion, f32[32,2,128]{2,1,0:T(2,128)} %mul.179), kind=kLoop, calls=%fused_computation.12 | loop fusion | flops 5242880 | bytes 8601600 | tf_op jit(solution)/shard_map/mul | solution.py:64
  85.7 8.7 %multiply_reduce_fusion = f32[2,128,128]{2,1,0:T(8,128)} fusion(f32[2,128,32,64]{1,0,3,2:T(2,128)S(1)} %reshape_reshape.12, f32[2,128,32,64]{1,0,3,2:T(2,128)S(1)} %copy-done.2, f32[32,2,128]{2,1,0:T(2,128)S(1)} %copy-done.11, f32[32,2,128]{2,1,0:T(2,128)S(1)} %copy.69, pred[128,128]{1,0:T(8,128)(4,1)S(1)} %iota_compare_fusion), kind=kOutput, calls=%fused_computation.10 | convolution fusion | flops 811565056 | bytes 4407296 | tf_op jit(solution)/shard_map/cahp,cbhp->hcab/dot_general | solution.py:93
  94.4 59.3 %all-gather.8.cloned.1.call-done = f32[256,64,128]{2,1,0:T(8,128)} async-done(((f32[32,64,128]{2,1,0:T(8,128)}), f32[256,64,128]{2,1,0:T(8,128)}) %all-gather.8.cloned.1.call-update) | async-done | bytes 8388624 | tf_op jit(solution)/shard_map/all_gather | solution.py:14
  153.7 27.7 %while.31 = (s32[]{:T(128)}, f32[32,64,128]{2,1,0:T(8,128)}, s32[]{:T(128)}, f32[8,32,64,128]{3,2,1,0:T(8,128)}, f32[8,32]{1,0:T(8,128)}, /*index=5*/s32[]{:T(128)}, s32[]{:T(128)}, s32[]{:T(128)}, s32[]{:T(128)}) while((s32[]{:T(128)}, f32[32,64,128]{2,1,0:T(8,128)}, s32[]{:T(128)}, f32[8,32,64,128]{3,2,1,0:T(8,128)}, ...), condition=%wide.region_6.7_spmd.clone, body=%wide.region_5.6_spmd.clone.sunk | while | flops 1048584 | bytes 3146279 | solution.py:27
  154.5 2.5 fusion.91
  157.6 2.8 fusion.91
  161.1 3.0 fusion.91
  164.8 2.8 fusion.91
  168.3 2.8 fusion.91
  171.7 2.8 fusion.91
  175.2 2.8 fusion.91
  178.6 2.8 fusion.91
  181.4 12.1 %multiply_add_fusion = f32[32,2,64,128]{3,1,2,0:T(2,128)S(1)} fusion(f32[32,2,64,128]{3,2,0,1:T(8,128)} %copy-done.8, f32[32,64,128]{2,1,0:T(8,128)} %get-tuple-element.231, f32[32,2]{1,0:T(8,128)S(1)} %copy-done.17, pred[2,2]{0,1:T(4,128)(4,1)S(1)} %copy-done.20, f32[32,2]{1,0:T(8,128)S(1)} %copy-done.15, f32[32,2]{1,0:T(8,128)S(1)} %copy-done.14, ...), kind=kOutput, calls=%fused_computation.22 | convolution fusion | flops 13632000 | bytes 5243908 | tf_op jit(solution)/shard_map/hkc,hkpn->hcpn/dot_general | solution.py:31
  193.6 4.2 %fusion.58 = f32[2,128,128]{2,1,0:T(8,128)} fusion(f32[32,2,64,128]{3,1,2,0:T(2,128)S(1)} %multiply_add_fusion, f32[2,128,32,64]{1,0,3,2:T(2,128)S(1)} %reshape_reshape.12, f32[2,128,32]{1,2,0:T(8,128)S(1)} %get-tuple-element.305), kind=kOutput, calls=%fused_computation.54 | convolution fusion | flops 805830656 | bytes 4358144 | tf_op jit(solution)/shard_map/jizk,zjky->jiy/dot_general | solution.py:31
  197.8 3.3 fusion.15
  201.0 77.5 %all-gather.6.cloned.1.call-done = f32[256,64,128]{2,1,0:T(8,128)} async-done(((f32[32,64,128]{2,1,0:T(8,128)}), f32[256,64,128]{2,1,0:T(8,128)}) %all-gather.6.cloned.1.call-update) | async-done | bytes 8388624 | tf_op jit(solution)/shard_map/all_gather | solution.py:14
  278.5 17.3 %while.30 = (s32[]{:T(128)}, f32[32,64,128]{2,1,0:T(8,128)S(1)}, s32[]{:T(128)}, f32[8,32]{1,0:T(8,128)}, f32[8,32,64,128]{3,2,1,0:T(8,128)}, /*index=5*/s32[]{:T(128)}, s32[]{:T(128)}) while((s32[]{:T(128)}, f32[32,64,128]{2,1,0:T(8,128)S(1)}, s32[]{:T(128)}, f32[8,32]{1,0:T(8,128)}, f32[8,32,64,128]{3,2,1,0:T(8,128)}, ...), condition=%wide.region_4.5_spmd.clone, body=%wide.region_3.4_spmd.clone.sunk | while | flops 1048580 | bytes 3146217 | solution.py:27
  279.2 1.5 fusion.90
  281.4 1.5 fusion.90
  283.6 1.5 fusion.90
  285.7 1.5 fusion.90
  287.9 1.5 fusion.90
  290.1 1.5 fusion.90
  292.2 1.5 fusion.90
  294.4 1.5 fusion.90
  295.9 13.5 %multiply_add_fusion.1 = f32[32,2,64,128]{3,1,2,0:T(2,128)S(1)} fusion(f32[32,2,64,128]{3,2,0,1:T(8,128)} %copy-done.7, f32[32,64,128]{2,1,0:T(8,128)S(1)} %get-tuple-element.230, f32[32,2]{1,0:T(8,128)S(1)} %copy-done.16, pred[2,2]{0,1:T(4,128)(4,1)S(1)} %copy-done.20, f32[32,2]{1,0:T(8,128)S(1)} %copy-done.15, f32[32,2]{1,0:T(8,128)S(1)} %copy-done.14, ...), kind=kOutput, calls=%fused_computation.23 | convolution fusion | flops 13632000 | bytes 5243908 | tf_op jit(solution)/shard_map/hck,hkpn->hcpn/dot_general | solution.py:31
  309.4 3.6 fusion.53
  313.0 3.2 fusion.19
  318.2 5.5 %fusion.8 = f32[2,128,32,64]{1,3,2,0:T(8,128)} fusion(f32[2,32,64,128]{3,2,1,0:T(8,128)S(1)} %copy-done.5, f32[2,128,32,64]{1,0,3,2:T(2,128)S(1)} %copy-done.3, f32[32,2,128,128]{3,2,1,0:T(8,128)S(1)} %copy-done.4, f32[2,128,32]{1,2,0:T(8,128)S(1)} %copy-done.13, f32[32]{0:T(128)S(1)} %copy-done.18, f32[2,128,32]{1,2,0:T(8,128)S(1)} %get-tuple-element.305), kind=kOutput, calls=%fused_computation.15 | convolution fusion | flops 807927808 | bytes 10551424 | tf_op jit(solution)/shard_map/hcst,cshp->cthp/dot_general | solution.py:31
  323.7 5.5 %copy.118 = f32[2,128,32,64]{3,2,1,0:T(8,128)} copy(f32[2,128,32,64]{1,3,2,0:T(8,128)} %fusion.8) | data formatting | bytes 4194304
  329.2 5.2 %reshape.109 = f32[256,2048]{1,0:T(8,128)} reshape(f32[2,128,32,64]{3,2,1,0:T(8,128)} %copy.118) | data formatting | bytes 4194304
  334.5 11.1 %fusion.10 = f32[2,128,32,64]{1,3,2,0:T(8,128)} fusion(f32[2,32,64,128]{3,2,1,0:T(8,128)} %fusion.19, f32[2,128,32,64]{1,0,3,2:T(2,128)S(1)} %reshape_reshape.12, f32[32,2,128,128]{3,2,1,0:T(8,128)} %get-tuple-element.303, f32[32]{0:T(128)S(1)} %copy-done.18, f32[2,128,32]{1,2,0:T(8,128)S(1)} %get-tuple-element.304), kind=kOutput, calls=%fused_computation.19 | convolution fusion | flops 807403520 | bytes 10518656 | tf_op jit(solution)/shard_map/hcts,cshp->cthp/dot_general | solution.py:31
  345.6 5.5 %copy.117 = f32[2,128,32,64]{3,2,1,0:T(8,128)} copy(f32[2,128,32,64]{1,3,2,0:T(8,128)} %fusion.10) | data formatting | bytes 4194304
  351.1 5.0 %reshape.108 = f32[256,2048]{1,0:T(8,128)} reshape(f32[2,128,32,64]{3,2,1,0:T(8,128)} %copy.117) | data formatting | bytes 4194304
  356.1 1.6 copy.207
  357.6 1.6 copy.208
  (92 shorter events, 24.9 us)
Async XLA Ops:
  7.2 7.9 %copy-start = (f32[256,128]{1,0:T(8,128)S(1)}, f32[256,128]{1,0:T(8,128)}, u32[]{:S(2)}) copy-start(f32[256,128]{1,0:T(8,128)} %param.16) | copy-start | bytes 393220
  7.2 146.5 %all-gather.8.cloned.1.call-start = ((), (), s32[]{:S(2)}) async-start(), calls=%async_computation.1 | async-start | bytes 9437184 | tf_op jit(solution)/shard_map/all_gather | solution.py:14
  14.9 2.1 copy-start.1
  17.0 9.0 %copy-start.8 = (f32[32,2,64,128]{3,2,0,1:T(8,128)}, f32[32,2,64,128]{3,2,0,1:T(8,128)S(1)}, u32[]{:S(2)}) copy-start(f32[32,2,64,128]{3,2,0,1:T(8,128)S(1)} %fusion.44) | copy-start | bytes 6291460
  26.0 252.5 %all-gather.6.cloned.1.call-start = ((), (), s32[]{:S(2)}) async-start(), calls=%async_computation | async-start | bytes 9437184 | tf_op jit(solution)/shard_map/all_gather | solution.py:14
  29.1 3.0 copy-start.6
  34.1 1.3 copy-start.7
  35.4 11.1 %copy-start.12 = (f32[32,256]{1,0:T(8,128)S(1)}, f32[32,256]{1,0:T(8,128)}, u32[]{:S(2)}) copy-start(f32[32,256]{1,0:T(8,128)} %param.12) | copy-start | bytes 98308
  35.4 11.7 %copy-start.19 = (u32[32]{0:T(128)S(1)}, u32[32]{0:T(128)}, u32[]{:S(2)}) copy-start(u32[32]{0:T(128)} %constant.83) | copy-start | bytes 388
  44.4 311.7 %all-reduce.4.cloned.1.call-start = ((), (), s32[]{:S(2)}) async-start(), calls=%async_computation.2 | async-start | bytes 524288 | tf_op jit(solution)/shard_map/psum | solution.py:148
  80.7 4.9 %copy-start.2 = (f32[2,128,32,64]{1,0,3,2:T(2,128)S(1)}, f32[2,128,32,64]{1,0,3,2:T(2,128)}, u32[]{:S(2)}) copy-start(f32[2,128,32,64]{1,0,3,2:T(2,128)} %copy-done.1) | copy-start | bytes 6291460
  80.8 4.9 %copy-start.11 = (f32[32,2,128]{2,1,0:T(2,128)S(1)}, f32[32,2,128]{2,1,0:T(2,128)}, u32[]{:S(2)}) copy-start(f32[32,2,128]{2,1,0:T(2,128)} %mul.179) | copy-start | bytes 98308
  153.7 27.7 %copy-start.14 = (f32[32,2]{1,0:T(8,128)S(1)}, f32[32,2]{1,0:T(8,128)}, u32[]{:S(2)}) copy-start(f32[32,2]{1,0:T(8,128)} %copy.76) | copy-start | bytes 772
  153.7 27.7 %copy-start.15 = (f32[32,2]{1,0:T(8,128)S(1)}, f32[32,2]{1,0:T(8,128)}, u32[]{:S(2)}) copy-start(f32[32,2]{1,0:T(8,128)} %copy.77) | copy-start | bytes 772
  153.7 27.7 %copy-start.17 = (f32[32,2]{1,0:T(8,128)S(1)}, f32[32,2]{1,0:T(8,128)}, u32[]{:S(2)}) copy-start(f32[32,2]{1,0:T(8,128)} %copy.92) | copy-start | bytes 772
  153.7 27.7 %copy-start.20 = (pred[2,2]{0,1:T(4,128)(4,1)S(1)}, pred[2,2]{0,1:T(4,128)(4,1)}, u32[]{:S(2)}) copy-start(pred[2,2]{0,1:T(4,128)(4,1)} %iota_compare_fusion.1) | copy-start | bytes 16
  278.5 17.3 %copy-start.16 = (f32[32,2]{1,0:T(8,128)S(1)}, f32[32,2]{1,0:T(8,128)}, u32[]{:S(2)}) copy-start(f32[32,2]{1,0:T(8,128)} %copy.82) | copy-start | bytes 772
  295.9 13.5 %copy-start.3 = (f32[2,128,32,64]{1,0,3,2:T(2,128)S(1)}, f32[2,128,32,64]{1,0,3,2:T(2,128)}, u32[]{:S(2)}) copy-start(f32[2,128,32,64]{1,0,3,2:T(2,128)} %copy-done.1) | copy-start | bytes 6291460
  309.4 6.8 %copy-start.10 = (f32[2,128,128]{2,1,0:T(8,128)S(1)}, f32[2,128,128]{2,1,0:T(8,128)}, u32[]{:S(2)}) copy-start(f32[2,128,128]{2,1,0:T(8,128)} %multiply_reduce_fusion) | copy-start | bytes 393220
  309.4 8.8 %copy-start.5 = (f32[2,32,64,128]{3,2,1,0:T(8,128)S(1)}, f32[2,32,64,128]{3,2,1,0:T(8,128)}, u32[]{:S(2)}) copy-start(f32[2,32,64,128]{3,2,1,0:T(8,128)} %fusion.15) | copy-start | bytes 6291460
  313.0 3.2 copy-start.9
  313.0 5.2 %copy-start.4 = (f32[32,2,128,128]{3,2,1,0:T(8,128)S(1)}, f32[32,2,128,128]{3,2,1,0:T(8,128)}, u32[]{:S(2)}) copy-start(f32[32,2,128,128]{3,2,1,0:T(8,128)} %get-tuple-element.302) | copy-start | bytes 12582916
  313.0 5.2 %copy-start.13 = (f32[2,128,32]{1,2,0:T(8,128)S(1)}, f32[2,128,32]{1,2,0:T(8,128)}, u32[]{:S(2)}) copy-start(f32[2,128,32]{1,2,0:T(8,128)} %copy.89) | copy-start | bytes 98308
  313.0 5.2 %copy-start.18 = (f32[32]{0:T(128)S(1)}, f32[32]{0:T(128)}, u32[]{:S(2)}) copy-start(f32[32]{0:T(128)} %param.14) | copy-start | bytes 388
Sparse Core Ops, SparseCore 0:
  26.1 127.5 all-gather.7
  155.8 122.6 all-gather.5
  334.6 16.4 all-reduce.3
where the time goes:
time: 373 us; the launch traced here: 366 us
  waiting for transfers between devices  137 us (37%)
  matrix products  89.2 us (24%)
  local copies, waits for them, and re-layouts  56 us (15%)
  other arithmetic  43.8 us (12%)
  blocking collectives  24.7 us (7%)
  between operations  15.1 us (4%)
    all_gather x2, waiting for transfers between devices, carried_in(): everything = jax.tree.map(lambda part: lax.all_gather(part, axis), array)  137 us
    dot_general x15, matrix products, mixed_output(): return jnp.einsum(form, left, right, precision=HIGH)  80.5 us
    select_n x16, other arithmetic, turn(): return jax.tree.map(lambda a, b: jnp.where(reached, a, b), new, before)  33.8 us
    unnamed x53, local copies, waits for them, and re-layouts  32.2 us
    unnamed x1, blocking collectives  24.7 us
    dot_general x1, matrix products, layer(): products = jnp.einsum('cahp,cbhp->hcab', dys, input_rows, precision=HIGH)  8.73 us
  transfers between devices with their start and end apart: 3, of which 2 were waited for; matrix products, arithmetic and copies ran while one was open for 30% of the time, Pallas kernels for 0%

commit v1 on v0

v1 whole, which is shorter than its diff:
```python
import functools

import jax
import jax.numpy as jnp
from jax import lax
from jax.experimental import pallas as pl
from jax.experimental.pallas import tpu as pltpu
from jax.sharding import PartitionSpec as P

HIGH = lax.Precision.HIGHEST
MESH = pl.DeviceIdType.MESH
F32, BF16 = jnp.float32, jnp.bfloat16
LANES = 128
COLS = 256
LAG = 2

NN = (((1,), (0,)), ((), ()))
NT = (((1,), (1,)), ((), ()))


def split(a):
    hi = a.astype(BF16)
    return hi, (a - hi.astype(F32)).astype(BF16)


def dot3(a, b, dims=NN):
    def one(l, r):
        return lax.dot_general(l, r, dims, preferred_element_type=F32)

    return one(a[0], b[0]) + one(a[0], b[1]) + one(a[1], b[0])


def kernel(
    n, nh, x_ref, rates_ref, decay_ref, skip_ref, b_ref, c_ref, dy_ref,
    out_ref, gx_ref, db_ref, dc_ref,
    u_ref, v_ref, vxh, vxl, udh, udl, ft, gt, e_in, a_in, dl_ref, sl_ref, m_ref,
    low_ref, part, got, send_f, recv_f, send_b, recv_b, send_h, recv_h,
):
    grp, me, head = lax.axis_index("grp"), lax.axis_index("seq"), lax.axis_index("head")
    tokens, width = x_ref.shape
    heads = rates_ref.shape[0]
    size = width // heads
    steps = width // COLS
    chunks = width // LANES
    per = COLS // LANES
    has_left, has_right = me > 0, me < n - 1
    barrier = pltpu.get_barrier_semaphore()

    @pl.when(has_left)
    def _():
        pl.semaphore_signal(barrier, inc=1, device_id=(grp, me - 1, head), device_id_type=MESH)

    @pl.when(has_right)
    def _():
        pl.semaphore_signal(barrier, inc=1, device_id=(grp, me + 1, head), device_id_type=MESH)

    for k in range(1, nh):
        other = lax.rem(head + k, nh)
        pl.semaphore_signal(barrier, inc=1, device_id=(grp, me, other), device_id_type=MESH)

    rows = lax.broadcasted_iota(jnp.int32, (tokens, tokens), 0)
    cols = lax.broadcasted_iota(jnp.int32, (tokens, tokens), 1)
    lower = jnp.where(rows >= cols, 1.0, 0.0).astype(F32)
    step_t = rates_ref[...].T
    cum = jnp.dot(lower, -(step_t * decay_ref[...]), precision=HIGH, preferred_element_type=F32)
    u = split(jnp.exp(cum))
    v = split(jnp.exp(-cum) * step_t)
    extra = jnp.concatenate(
        [
            jnp.broadcast_to(jnp.exp(cum[tokens - 1 :, :]), (8, heads)),
            jnp.broadcast_to(skip_ref[...], (8, heads)),
        ],
        axis=0,
    )
    extra_hi = extra.astype(BF16)
    extra_mid, extra_lo = split(extra - extra_hi.astype(F32))
    bt = split(b_ref[...].T)
    ct = split(c_ref[...].T)
    b_s, c_s = split(b_ref[...]), split(c_ref[...])
    low = split(jnp.where(rows >= cols, dot3(c_s, b_s, NT), 0.0))
    upp = split(jnp.where(rows <= cols, dot3(b_s, c_s, NT), 0.0))
    low_ref[0], low_ref[1] = low
    low_ref[2], low_ref[3] = upp

    def prepare(k, _):
        at = pl.ds(pl.multiple_of(k * COLS, COLS), COLS)
        lane = lax.broadcasted_iota(jnp.int32, (heads, COLS), 1) + k * COLS
        row = lax.broadcasted_iota(jnp.int32, (heads, COLS), 0)
        spread = jnp.where((lane >= row * size) & (lane < (row + 1) * size), 1.0, 0.0).astype(BF16)

        def wide(*terms):
            return sum(jnp.dot(t, spread, preferred_element_type=F32) for t in terms)

        u_w, v_w, e_w = wide(*u), wide(*v), wide(extra_hi, extra_mid, extra_lo)
        u_ref[:, at] = u_w
        v_ref[:, at] = v_w
        dl_ref[:, at] = e_w[:8]
        sl_ref[:, at] = e_w[8:]
        vx = split(v_w * x_ref[:, at])
        ud = split(u_w * dy_ref[:, at])
        vxh[:, at], vxl[:, at] = vx
        udh[:, at], udl[:, at] = ud
        f = dot3(bt, vx) * e_w[:1]
        g = dot3(ct, ud)
        for i in range(per):
            ft[k * per + i] = f[:, i * LANES : (i + 1) * LANES]
            gt[k * per + i] = g[:, i * LANES : (i + 1) * LANES]
        return 0

    lax.fori_loop(0, steps, prepare, 0)
    m_ref[...] = jnp.zeros_like(m_ref)

    @pl.when(jnp.logical_not(has_left))
    def _():
        e_in[...] = jnp.zeros_like(e_in)

    @pl.when(jnp.logical_not(has_right))
    def _():
        a_in[...] = jnp.zeros_like(a_in)

    peers = has_left.astype(jnp.int32) + has_right.astype(jnp.int32) + nh - 1
    pl.semaphore_wait(barrier, peers)

    def ahead(k):
        return pltpu.make_async_remote_copy(
            src_ref=ft.at[k], dst_ref=e_in.at[k], send_sem=send_f.at[k], recv_sem=recv_f.at[k],
            device_id=(grp, me + 1, head), device_id_type=MESH,
        )

    def behind(k):
        return pltpu.make_async_remote_copy(
            src_ref=gt.at[k], dst_ref=a_in.at[k], send_sem=send_b.at[k], recv_sem=recv_b.at[k],
            device_id=(grp, me - 1, head), device_id_type=MESH,
        )

    def relay(k, copy, before, after, incoming, own):
        @pl.when(before)
        def _():
            copy(k).wait_recv()

            @pl.when(after)
            def _():
                d = dl_ref[:1, pl.ds(pl.multiple_of(k * LANES, LANES), LANES)]
                own[k] = own[k] + d * incoming[k]

        @pl.when(after)
        def _():
            copy(k).start()

    def inner(k):
        at = pl.ds(pl.multiple_of(k * COLS, COLS), COLS)
        vx = vxh[:, at], vxl[:, at]
        ud = udh[:, at], udl[:, at]
        out_ref[:, at] = dot3((low_ref[0], low_ref[1]), vx)
        gx_ref[:, at] = dot3((low_ref[2], low_ref[3]), ud)
        m_ref[...] += dot3(ud, vx, NT)

    def turn(s, _):
        f = s - me * LAG
        b = s - (n - 1 - me) * LAG

        @pl.when((f >= 0) & (f < chunks))
        def _():
            relay(f, ahead, has_left, has_right, e_in, ft)

        @pl.when((b >= 0) & (b < chunks))
        def _():
            relay(b, behind, has_right, has_left, a_in, gt)

        @pl.when(s < steps)
        def _():
            inner(s)

        return 0

    lax.fori_loop(0, max(steps, chunks + (n - 1) * LAG), turn, 0)

    m = jnp.where(rows >= cols, m_ref[...], 0.0)
    part[0] = dot3(split(m.T), c_s)
    part[1] = dot3(split(m), b_s)

    def finish(k, _):
        at = pl.ds(pl.multiple_of(k * COLS, COLS), COLS)
        e = split(jnp.concatenate([e_in[k * per + i] for i in range(per)], axis=1))
        a = split(jnp.concatenate([a_in[k * per + i] for i in range(per)], axis=1) * dl_ref[:1, at])
        skip_w = sl_ref[:1, at]
        out_ref[:, at] = u_ref[:, at] * (out_ref[:, at] + dot3(c_s, e)) + skip_w * x_ref[:, at]
        gx_ref[:, at] = v_ref[:, at] * (gx_ref[:, at] + dot3(b_s, a)) + skip_w * dy_ref[:, at]
        part[0] += dot3((vxh[:, at], vxl[:, at]), a, NT)
        part[1] += dot3((udh[:, at], udl[:, at]), e, NT)
        return 0

    lax.fori_loop(0, steps, finish, 0)

    def across(k):
        return pltpu.make_async_remote_copy(
            src_ref=part, dst_ref=got.at[k - 1], send_sem=send_h.at[k - 1], recv_sem=recv_h.at[k - 1],
            device_id=(grp, me, lax.rem(head + k, nh)), device_id_type=MESH,
        )

    for k in range(1, nh):
        across(k).start()

    def drain(k, _):
        @pl.when(has_right)
        def _():
            ahead(k).wait_send()

        @pl.when(has_left)
        def _():
            behind(k).wait_send()

        return 0

    lax.fori_loop(0, chunks, drain, 0)
    total_b, total_c = part[0], part[1]
    for k in range(1, nh):
        across(k).wait()
        total_b += got[k - 1, 0]
        total_c += got[k - 1, 1]
    db_ref[...] = total_b
    dc_ref[...] = total_c


def body(n, nh, inputs, rates, decay_rate, skip, keys_b, keys_c, grad_out):
    tokens, width = inputs.shape
    heads = rates.shape[0]
    state = keys_b.shape[1]
    chunks = width // LANES
    vmem = pl.BlockSpec(memory_space=pltpu.VMEM)
    dma = pltpu.SemaphoreType.DMA
    others = max(nh - 1, 1)
    return pl.pallas_call(
        functools.partial(kernel, n, nh),
        out_shape=(
            jax.ShapeDtypeStruct((tokens, width), F32),
            jax.ShapeDtypeStruct((tokens, width), F32),
            jax.ShapeDtypeStruct((tokens, state), F32),
            jax.ShapeDtypeStruct((tokens, state), F32),
        ),
        in_specs=[vmem] * 7,
        out_specs=(vmem,) * 4,
        scratch_shapes=[
            pltpu.VMEM((tokens, width), F32),
            pltpu.VMEM((tokens, width), F32),
            pltpu.VMEM((tokens, width), BF16),
            pltpu.VMEM((tokens, width), BF16),
            pltpu.VMEM((tokens, width), BF16),
            pltpu.VMEM((tokens, width), BF16),
            pltpu.VMEM((chunks, state, LANES), F32),
            pltpu.VMEM((chunks, state, LANES), F32),
            pltpu.VMEM((chunks, state, LANES), F32),
            pltpu.VMEM((chunks, state, LANES), F32),
            pltpu.VMEM((8, width), F32),
            pltpu.VMEM((8, width), F32),
            pltpu.VMEM((tokens, tokens), F32),
            pltpu.VMEM((4, tokens, tokens), BF16),
            pltpu.VMEM((2, tokens, state), F32),
            pltpu.VMEM((others, 2, tokens, state), F32),
            dma((chunks,)),
            dma((chunks,)),
            dma((chunks,)),
            dma((chunks,)),
            dma((others,)),
            dma((others,)),
        ],
        compiler_params=pltpu.CompilerParams(collective_id=0, has_side_effects=True),
        name="mixer",
    )(inputs, rates, decay_rate[None, :], skip[None, :], keys_b, keys_c, grad_out)


def solution(mesh):
    in_specs = (
        P(("grp", "seq"), "head"),
        P("head", ("grp", "seq")),
        P("head"),
        P("head"),
        P(("grp", "seq"), None),
        P(("grp", "seq"), None),
        P(("grp", "seq"), "head"),
    )
    out_specs = (
        P(("grp", "seq"), "head"),
        P(("grp", "seq"), "head"),
        P(("grp", "seq"), None),
        P(("grp", "seq"), None),
    )
    run = functools.partial(body, mesh.shape["seq"], mesh.shape["head"])
    return jax.shard_map(run, mesh=mesh, in_specs=in_specs, out_specs=out_specs, check_vma=False)
```

time: 373 us -> 93.4 us (0.25); the launches traced: 366 us -> 93.2 us
  waiting for transfers between devices: 137 us -> 0 us
  matrix products: 89.2 us -> 0 us
  Pallas kernels: 0 us -> 86.7 us
  local copies, waits for them, and re-layouts: 56 us -> 5.93 us
  other arithmetic: 43.8 us -> 0 us
  blocking collectives: 24.7 us -> 0 us
  between operations: 15.1 us -> 0.65 us
    all_gather x2 -> x0, waiting for transfers between devices: 137 us -> none  [carried_in(): everything = jax.tree.map(lambda part: lax.all_gather(part, axis), array)]
    dot_general x16 -> x0, matrix products: 89.2 us -> none  [the longest x15 80.5 us: mixed_output(): return jnp.einsum(form, left, right, precision=HIGH)]
    pallas_call x0 -> x1, Pallas kernels: none -> 86.7 us  [body(): pl.pallas_call(functools.partial(kernel, n, nh), out_shape=(jax.ShapeDtyp...]
    select_n x16 -> x0, other arithmetic: 33.8 us -> none  [turn(): return jax.tree.map(lambda a, b: jnp.where(reached, a, b), new, before)]
    unnamed x53 -> x10, local copies, waits for them, and re-layouts: 32.2 us -> 5.93 us
    unnamed x1 -> x0, blocking collectives: 24.7 us -> none
    mul x17 -> x0, local copies, waits for them, and re-layouts: 11.7 us -> none  [the longest x8 5.54 us: join_forward(): later[0][:, None, None] * earlier[1] + later[1]]
    another operation x4 -> x0, local copies, waits for them, and re-layouts: 5.35 us -> none  [the longest x1 2.33 us: layer(): input_rows = inputs.reshape(count, block, heads, width)]
  transfers between devices with their start and end apart: 3 -> 0, of which waited for: 2 -> 0; matrix products, arithmetic and copies ran while one was open for 30% -> 0% of each run, Pallas kernels for 0% -> 0%
where the time goes in v1:
time: 93.4 us; the launch traced here: 93.2 us
  Pallas kernels  86.7 us (93%)
  local copies, waits for them, and re-layouts  5.93 us (6%)
    pallas_call x1, Pallas kernels, body(): pl.pallas_call(functools.partial(kernel, n, nh), out_shape=(jax.ShapeDtyp...  86.7 us
    unnamed x10, local copies, waits for them, and re-layouts  5.93 us

profile of v1, /device:TPU:0, one launch (start us, length us, event | category | flops | bytes accessed | tf_op | source)
XLA Modules:
  0.0 93.2 jit_solution(15547969777485766586)
XLA Ops:
  0.6 86.7 %mixer.1 = (f32[256,2048]{1,0:T(8,128)}, f32[256,2048]{1,0:T(8,128)}, f32[256,128]{1,0:T(8,128)}, f32[256,128]{1,0:T(8,128)}) custom-call(f32[256,2048]{1,0:T(8,128)} %x_ref.1, f32[32,256]{1,0:T(8,128)} %rates_ref.1, f32[1,32]{1,0:T(1,128)} %bitcast.2, f32[1,32]{1,0:T(1,128)} %bitcast.3, f32[256,128]{1,0:T(8,128)} %b_ref.1, f32[256,128]{1,0:T(8,128)} %c_ref.1, ...), custom_call_target="tpu_custom_call" | custom-call | tf_op jit(solution)/shard_map/mixer/pallas_call | solution.py:233
  87.3 0.0 copy-start
  87.3 3.3 %copy.15 = f32[256,2048]{1,0:T(8,128)} copy(f32[256,2048]{1,0:T(8,128)} %get-tuple-element.8) | data formatting | bytes 4194304
  90.6 0.0 copy-done
  90.6 0.0 copy-start.2
  90.6 0.0 copy-start.1
  90.6 1.3 %copy.16 = f32[256,2048]{1,0:T(8,128)} copy(f32[256,2048]{1,0:T(8,128)S(1)} %copy-done) | data formatting | bytes 4194304
  91.9 0.0 copy-done.2
  91.9 0.7 copy.17
  92.6 0.0 copy-done.1
  92.6 0.7 copy.18
Async XLA Ops:
  87.3 3.3 %copy-start = (f32[256,2048]{1,0:T(8,128)S(1)}, f32[256,2048]{1,0:T(8,128)}, u32[]{:S(2)}) copy-start(f32[256,2048]{1,0:T(8,128)} %get-tuple-element.9) | copy-start | bytes 6291460
  90.6 1.3 %copy-start.2 = (f32[256,128]{1,0:T(8,128)S(1)}, f32[256,128]{1,0:T(8,128)}, u32[]{:S(2)}) copy-start(f32[256,128]{1,0:T(8,128)} %get-tuple-element.10) | copy-start | bytes 393220
  90.6 2.0 %copy-start.1 = (f32[256,128]{1,0:T(8,128)S(1)}, f32[256,128]{1,0:T(8,128)}, u32[]{:S(2)}) copy-start(f32[256,128]{1,0:T(8,128)} %get-tuple-element.11) | copy-start | bytes 393220

commit v2 on v1

v2 whole, which is shorter than its diff:
```python
import functools

import jax
import jax.numpy as jnp
from jax import lax
from jax.experimental import pallas as pl
from jax.experimental.pallas import tpu as pltpu
from jax.sharding import PartitionSpec as P

HIGH = lax.Precision.HIGHEST
MESH = pl.DeviceIdType.MESH
F32, BF16 = jnp.float32, jnp.bfloat16
LANES = 128
COLS = 256

NN = (((1,), (0,)), ((), ()))
NT = (((1,), (1,)), ((), ()))


def split(a):
    hi = a.astype(BF16)
    return hi, (a - hi.astype(F32)).astype(BF16)


def dot3(a, b, dims=NN):
    def one(l, r):
        return lax.dot_general(l, r, dims, preferred_element_type=F32)

    return one(a[0], b[0]) + one(a[0], b[1]) + one(a[1], b[0])


def split3(a):
    hi = a.astype(BF16)
    return (hi,) + split(a - hi.astype(F32))


def kernel(
    n, nh, x_ref, rates_ref, decay_ref, skip_ref, b_ref, c_ref, dy_ref,
    out_ref, gx_ref, db_ref, dc_ref,
    u_ref, v_ref, vxh, vxl, udh, udl, near, own, got_near, got_chain, got_back,
    tot_ref, tot_in, dl_ref, sl_ref, pl_ref, m_ref, low_ref, part, got,
    send_n, recv_n, send_c, recv_c, send_j, recv_j, send_h, recv_h, send_t, recv_t,
):
    grp, me, head = lax.axis_index("grp"), lax.axis_index("seq"), lax.axis_index("head")
    tokens, width = x_ref.shape
    heads = rates_ref.shape[0]
    size = width // heads
    steps = width // COLS
    chunks = width // LANES
    per = COLS // LANES
    late = lax.rem(me, 2)
    forward = late == 1
    mate = me + 1 - 2 * late
    stride = 4 * late - 2
    first, last = me < 2, me >= n - 2
    has_in = (forward & jnp.logical_not(first)) | (jnp.logical_not(forward) & jnp.logical_not(last))
    has_out = (forward & jnp.logical_not(last)) | (jnp.logical_not(forward) & jnp.logical_not(first))
    barrier = pltpu.get_barrier_semaphore()

    def greet(seq, core):
        pl.semaphore_signal(barrier, inc=1, device_id=(grp, seq, core), device_id_type=MESH)

    greet(mate, head)

    @pl.when(has_in)
    def _():
        greet(me - stride, head)

    @pl.when(has_out)
    def _():
        greet(me + stride, head)

    for k in range(1, nh):
        greet(me, lax.rem(head + k, nh))

    rows = lax.broadcasted_iota(jnp.int32, (tokens, tokens), 0)
    cols = lax.broadcasted_iota(jnp.int32, (tokens, tokens), 1)
    lower = jnp.where(rows >= cols, 1.0, 0.0).astype(F32)
    step_t = rates_ref[...].T
    cum = jnp.dot(lower, -(step_t * decay_ref[...]), precision=HIGH, preferred_element_type=F32)
    u = split(jnp.exp(cum))
    v = split(jnp.exp(-cum) * step_t)
    tot_ref[...] = jnp.broadcast_to(jnp.exp(cum[tokens - 1 :, :]), (8, heads))
    extra = split3(
        jnp.concatenate([tot_ref[...], jnp.broadcast_to(skip_ref[...], (8, heads))], axis=0)
    )
    b_s, c_s = split(b_ref[...]), split(c_ref[...])
    bt = split(b_ref[...].T)
    ct = split(c_ref[...].T)

    def spread(k):
        lane = lax.broadcasted_iota(jnp.int32, (heads, COLS), 1) + k * COLS
        row = lax.broadcasted_iota(jnp.int32, (heads, COLS), 0)
        return jnp.where((lane >= row * size) & (lane < (row + 1) * size), 1.0, 0.0).astype(BF16)

    def wide(k, terms):
        return sum(jnp.dot(t, spread(k), preferred_element_type=F32) for t in terms)

    def columns(k):
        return pl.ds(pl.multiple_of(k * COLS, COLS), COLS)

    def lanes(k):
        return pl.ds(pl.multiple_of(k * LANES, LANES), LANES)

    def remote(src, dst, sends, recvs, k, to):
        return pltpu.make_async_remote_copy(
            src_ref=src.at[k], dst_ref=dst.at[k], send_sem=sends.at[k], recv_sem=recvs.at[k],
            device_id=(grp, to, head), device_id_type=MESH,
        )

    def to_mate(k):
        return remote(near, got_near, send_n, recv_n, k, mate)

    def onward(k):
        return remote(own, got_chain, send_c, recv_c, k, me + stride)

    def back(k):
        return remote(got_chain, got_back, send_j, recv_j, k, mate)

    total_to_mate = pltpu.make_async_remote_copy(
        src_ref=tot_ref, dst_ref=tot_in, send_sem=send_t.at[0], recv_sem=recv_t.at[0],
        device_id=(grp, mate, head), device_id_type=MESH,
    )
    amount = has_in.astype(jnp.int32) + has_out.astype(jnp.int32) + nh
    pl.semaphore_wait(barrier, amount)
    total_to_mate.start()

    def prepare(k, _):
        at = columns(k)
        u_w, v_w, e_w = wide(k, u), wide(k, v), wide(k, extra)
        u_ref[:, at] = u_w
        v_ref[:, at] = v_w
        dl_ref[:, at] = e_w[:8]
        sl_ref[:, at] = e_w[8:]
        vx = split(v_w * x_ref[:, at])
        ud = split(u_w * dy_ref[:, at])
        vxh[:, at], vxl[:, at] = vx
        udh[:, at], udl[:, at] = ud
        f = dot3(bt, vx) * e_w[:1]
        g = dot3(ct, ud)
        to, keep = jnp.where(forward, g, f), jnp.where(forward, f, g)
        for i in range(per):
            near[k * per + i] = to[:, i * LANES : (i + 1) * LANES]
            own[k * per + i] = keep[:, i * LANES : (i + 1) * LANES]
        for i in range(per):
            to_mate(k * per + i).start()
        return 0

    lax.fori_loop(0, steps, prepare, 0)
    low_ref[0], low_ref[1] = split(jnp.where(rows >= cols, dot3(c_s, b_s, NT), 0.0))
    low_ref[2], low_ref[3] = split(jnp.where(rows <= cols, dot3(b_s, c_s, NT), 0.0))
    m_ref[...] = jnp.zeros_like(m_ref)
    part[...] = jnp.zeros_like(part)
    total_to_mate.wait_recv()
    mates = split3(tot_in[...])

    def inner(k):
        at = columns(k)
        vx = vxh[:, at], vxl[:, at]
        ud = udh[:, at], udl[:, at]
        out_ref[:, at] = dot3((low_ref[0], low_ref[1]), vx)
        gx_ref[:, at] = dot3((low_ref[2], low_ref[3]), ud)
        m_ref[...] += dot3(ud, vx, NT)

    def gather(ref, k):
        return jnp.concatenate([ref[k * per + i] for i in range(per)], axis=1)

    def finish_out(ref, k):
        at = columns(k)
        e = split(gather(ref, k))
        out_ref[:, at] = u_ref[:, at] * (out_ref[:, at] + dot3(c_s, e)) + sl_ref[:1, at] * x_ref[:, at]
        part[1] += dot3((udh[:, at], udl[:, at]), e, NT)

    def finish_gx(ref, k):
        at = columns(k)
        a = split(gather(ref, k) * dl_ref[:1, at])
        gx_ref[:, at] = v_ref[:, at] * (gx_ref[:, at] + dot3(b_s, a)) + sl_ref[:1, at] * dy_ref[:, at]
        part[0] += dot3((vxh[:, at], vxl[:, at]), a, NT)

    def chain(k, _):
        at = columns(k)
        inner(k)
        pl_ref[:, at] = wide(k, mates)
        for i in range(per):
            c = k * per + i
            to_mate(c).wait_recv()

            @pl.when(has_in)
            def _():
                onward(c).wait_recv()
                got_near[c] = got_near[c] + pl_ref[:1, lanes(c)] * got_chain[c]

            @pl.when(has_out)
            def _():
                own[c] = own[c] + dl_ref[:1, lanes(c)] * got_near[c]
                onward(c).start()

            @pl.when(has_in)
            def _():
                back(c).start()

        @pl.when(forward)
        def _():
            finish_out(got_near, k)

        @pl.when(jnp.logical_not(forward))
        def _():
            finish_gx(got_near, k)

        return 0

    lax.fori_loop(0, steps, chain, 0)
    m = jnp.where(rows >= cols, m_ref[...], 0.0)
    part[0] += dot3(split(m.T), c_s)
    part[1] += dot3(split(m), b_s)

    @pl.when(jnp.logical_not(has_out))
    def _():
        got_back[...] = jnp.zeros_like(got_back)

    def close(k, _):
        @pl.when(has_out)
        def _():
            for i in range(per):
                back(k * per + i).wait_recv()

        @pl.when(forward)
        def _():
            finish_gx(got_back, k)

        @pl.when(jnp.logical_not(forward))
        def _():
            finish_out(got_back, k)

        return 0

    lax.fori_loop(0, steps, close, 0)

    def across(k):
        return pltpu.make_async_remote_copy(
            src_ref=part, dst_ref=got.at[k - 1], send_sem=send_h.at[k - 1], recv_sem=recv_h.at[k - 1],
            device_id=(grp, me, lax.rem(head + k, nh)), device_id_type=MESH,
        )

    for k in range(1, nh):
        across(k).start()

    total_to_mate.wait_send()

    def drain(k, _):
        to_mate(k).wait_send()

        @pl.when(has_out)
        def _():
            onward(k).wait_send()

        @pl.when(has_in)
        def _():
            back(k).wait_send()

        return 0

    lax.fori_loop(0, chunks, drain, 0)
    total_b, total_c = part[0], part[1]
    for k in range(1, nh):
        across(k).wait()
        total_b += got[k - 1, 0]
        total_c += got[k - 1, 1]
    db_ref[...] = total_b
    dc_ref[...] = total_c


def body(n, nh, inputs, rates, decay_rate, skip, keys_b, keys_c, grad_out):
    tokens, width = inputs.shape
    heads = rates.shape[0]
    state = keys_b.shape[1]
    chunks = width // LANES
    vmem = pl.BlockSpec(memory_space=pltpu.VMEM)
    dma = pltpu.SemaphoreType.DMA
    others = max(nh - 1, 1)
    return pl.pallas_call(
        functools.partial(kernel, n, nh),
        out_shape=(
            jax.ShapeDtypeStruct((tokens, width), F32),
            jax.ShapeDtypeStruct((tokens, width), F32),
            jax.ShapeDtypeStruct((tokens, state), F32),
            jax.ShapeDtypeStruct((tokens, state), F32),
        ),
        in_specs=[vmem] * 7,
        out_specs=(vmem,) * 4,
        scratch_shapes=[
            pltpu.VMEM((tokens, width), F32),
            pltpu.VMEM((tokens, width), F32),
            pltpu.VMEM((tokens, width), BF16),
            pltpu.VMEM((tokens, width), BF16),
            pltpu.VMEM((tokens, width), BF16),
            pltpu.VMEM((tokens, width), BF16),
            pltpu.VMEM((chunks, state, LANES), F32),
            pltpu.VMEM((chunks, state, LANES), F32),
            pltpu.VMEM((chunks, state, LANES), F32),
            pltpu.VMEM((chunks, state, LANES), F32),
            pltpu.VMEM((chunks, state, LANES), F32),
            pltpu.VMEM((8, heads), F32),
            pltpu.VMEM((8, heads), F32),
            pltpu.VMEM((8, width), F32),
            pltpu.VMEM((8, width), F32),
            pltpu.VMEM((8, width), F32),
            pltpu.VMEM((tokens, tokens), F32),
            pltpu.VMEM((4, tokens, tokens), BF16),
            pltpu.VMEM((2, tokens, state), F32),
            pltpu.VMEM((others, 2, tokens, state), F32),
            dma((chunks,)),
            dma((chunks,)),
            dma((chunks,)),
            dma((chunks,)),
            dma((chunks,)),
            dma((chunks,)),
            dma((others,)),
            dma((others,)),
            dma((1,)),
            dma((1,)),
        ],
        compiler_params=pltpu.CompilerParams(collective_id=0, has_side_effects=True),
        name="mixer",
    )(inputs, rates, decay_rate[None, :], skip[None, :], keys_b, keys_c, grad_out)


def solution(mesh):
    in_specs = (
        P(("grp", "seq"), "head"),
        P("head", ("grp", "seq")),
        P("head"),
        P("head"),
        P(("grp", "seq"), None),
        P(("grp", "seq"), None),
        P(("grp", "seq"), "head"),
    )
    out_specs = (
        P(("grp", "seq"), "head"),
        P(("grp", "seq"), "head"),
        P(("grp", "seq"), None),
        P(("grp", "seq"), None),
    )
    run = functools.partial(body, mesh.shape["seq"], mesh.shape["head"])
    return jax.shard_map(run, mesh=mesh, in_specs=in_specs, out_specs=out_specs, check_vma=False)
```

time: 93.4 us -> 63.2 us (0.68)
  the two profiles are of different devices: /device:TPU:0 before, /device:TPU:9 now
where the time goes in v2:
time: 63.2 us; the launch traced here: 63 us
  Pallas kernels  56.5 us (89%)
  local copies, waits for them, and re-layouts  5.93 us (9%)
  between operations  0.65 us (1%)
    pallas_call x1, Pallas kernels, body(): pl.pallas_call(functools.partial(kernel, n, nh), out_shape=(jax.ShapeDtyp...  56.5 us
    unnamed x10, local copies, waits for them, and re-layouts  5.93 us

profile of v2, /device:TPU:9, one launch (start us, length us, event | category | flops | bytes accessed | tf_op | source)
XLA Modules:
  0.0 63.0 jit_solution(2102682198412941855)
XLA Ops:
  0.6 56.5 %mixer.1 = (f32[256,2048]{1,0:T(8,128)}, f32[256,2048]{1,0:T(8,128)}, f32[256,128]{1,0:T(8,128)}, f32[256,128]{1,0:T(8,128)}) custom-call(f32[256,2048]{1,0:T(8,128)} %x_ref.1, f32[32,256]{1,0:T(8,128)} %rates_ref.1, f32[1,32]{1,0:T(1,128)} %bitcast.2, f32[1,32]{1,0:T(1,128)} %bitcast.3, f32[256,128]{1,0:T(8,128)} %b_ref.1, f32[256,128]{1,0:T(8,128)} %c_ref.1, ...), custom_call_target="tpu_custom_call" | custom-call | tf_op jit(solution)/shard_map/mixer/pallas_call | solution.py:281
  57.1 0.0 copy-start
  57.1 3.3 %copy.15 = f32[256,2048]{1,0:T(8,128)} copy(f32[256,2048]{1,0:T(8,128)} %get-tuple-element.8) | data formatting | bytes 4194304
  60.4 0.0 copy-done
  60.4 0.0 copy-start.2
  60.4 0.0 copy-start.1
  60.4 1.3 %copy.16 = f32[256,2048]{1,0:T(8,128)} copy(f32[256,2048]{1,0:T(8,128)S(1)} %copy-done) | data formatting | bytes 4194304
  61.7 0.0 copy-done.2
  61.7 0.7 %copy.17 = f32[256,128]{1,0:T(8,128)} copy(f32[256,128]{1,0:T(8,128)S(1)} %copy-done.2) | data formatting | bytes 262144
  62.4 0.0 copy-done.1
  62.4 0.7 %copy.18 = f32[256,128]{1,0:T(8,128)} copy(f32[256,128]{1,0:T(8,128)S(1)} %copy-done.1) | data formatting | bytes 262144
Async XLA Ops:
  57.1 3.3 %copy-start = (f32[256,2048]{1,0:T(8,128)S(1)}, f32[256,2048]{1,0:T(8,128)}, u32[]{:S(2)}) copy-start(f32[256,2048]{1,0:T(8,128)} %get-tuple-element.9) | copy-start | bytes 6291460
  60.4 1.3 %copy-start.2 = (f32[256,128]{1,0:T(8,128)S(1)}, f32[256,128]{1,0:T(8,128)}, u32[]{:S(2)}) copy-start(f32[256,128]{1,0:T(8,128)} %get-tuple-element.10) | copy-start | bytes 393220
  60.4 2.0 %copy-start.1 = (f32[256,128]{1,0:T(8,128)S(1)}, f32[256,128]{1,0:T(8,128)}, u32[]{:S(2)}) copy-start(f32[256,128]{1,0:T(8,128)} %get-tuple-element.11) | copy-start | bytes 393220

commit v3 on v2

--- a/solution.py
+++ b/solution.py
@@ -11,6 +11,7 @@
 MESH = pl.DeviceIdType.MESH
 F32, BF16 = jnp.float32, jnp.bfloat16
 LANES = 128
+VMEM_BYTES = 67043328
 COLS = 256
 
 NN = (((1,), (0,)), ((), ()))
@@ -35,19 +36,27 @@
 
 
 def kernel(
-    n, nh, x_ref, rates_ref, decay_ref, skip_ref, b_ref, c_ref, dy_ref,
+    n, nh, x_hbm, rates_ref, decay_ref, skip_ref, b_ref, c_ref, dy_hbm,
     out_ref, gx_ref, db_ref, dc_ref,
-    u_ref, v_ref, vxh, vxl, udh, udl, near, own, got_near, got_chain, got_back,
+    x_ref, dy_ref, u_ref, v_ref, vxh, vxl, udh, udl, near, own, got_near, got_chain, got_back,
     tot_ref, tot_in, dl_ref, sl_ref, pl_ref, m_ref, low_ref, part, got,
-    send_n, recv_n, send_c, recv_c, send_j, recv_j, send_h, recv_h, send_t, recv_t,
+    send_n, recv_n, send_c, recv_c, send_j, recv_j, send_h, recv_h, send_t, recv_t, load_x, load_dy,
 ):
     grp, me, head = lax.axis_index("grp"), lax.axis_index("seq"), lax.axis_index("head")
-    tokens, width = x_ref.shape
+    tokens, width = x_hbm.shape
     heads = rates_ref.shape[0]
     size = width // heads
     steps = width // COLS
     chunks = width // LANES
     per = COLS // LANES
+
+    def load(src, dst, sems, k):
+        at = pl.ds(pl.multiple_of(k * COLS, COLS), COLS)
+        return pltpu.make_async_copy(src.at[:, at], dst.at[:, at], sems.at[k])
+
+    for k in range(steps):
+        load(x_hbm, x_ref, load_x, k).start()
+        load(dy_hbm, dy_ref, load_dy, k).start()
     late = lax.rem(me, 2)
     forward = late == 1
     mate = me + 1 - 2 * late
@@ -132,6 +141,8 @@
         v_ref[:, at] = v_w
         dl_ref[:, at] = e_w[:8]
         sl_ref[:, at] = e_w[8:]
+        load(x_hbm, x_ref, load_x, k).wait()
+        load(dy_hbm, dy_ref, load_dy, k).wait()
         vx = split(v_w * x_ref[:, at])
         ud = split(u_w * dy_ref[:, at])
         vxh[:, at], vxl[:, at] = vx
@@ -214,6 +225,16 @@
     part[0] += dot3(split(m.T), c_s)
     part[1] += dot3(split(m), b_s)
 
+    def across(k, which):
+        return pltpu.make_async_remote_copy(
+            src_ref=part.at[which], dst_ref=got.at[k - 1, which],
+            send_sem=send_h.at[k - 1, which], recv_sem=recv_h.at[k - 1, which],
+            device_id=(grp, me, lax.rem(head + k, nh)), device_id_type=MESH,
+        )
+
+    for k in range(1, nh):
+        across(k, late).start()
+
     @pl.when(jnp.logical_not(has_out))
     def _():
         got_back[...] = jnp.zeros_like(got_back)
@@ -236,14 +257,8 @@
 
     lax.fori_loop(0, steps, close, 0)
 
-    def across(k):
-        return pltpu.make_async_remote_copy(
-            src_ref=part, dst_ref=got.at[k - 1], send_sem=send_h.at[k - 1], recv_sem=recv_h.at[k - 1],
-            device_id=(grp, me, lax.rem(head + k, nh)), device_id_type=MESH,
-        )
-
     for k in range(1, nh):
-        across(k).start()
+        across(k, 1 - late).start()
 
     total_to_mate.wait_send()
 
@@ -263,7 +278,8 @@
     lax.fori_loop(0, chunks, drain, 0)
     total_b, total_c = part[0], part[1]
     for k in range(1, nh):
-        across(k).wait()
+        across(k, 0).wait()
+        across(k, 1).wait()
         total_b += got[k - 1, 0]
         total_c += got[k - 1, 1]
     db_ref[...] = total_b
@@ -276,19 +292,24 @@
     state = keys_b.shape[1]
     chunks = width // LANES
     vmem = pl.BlockSpec(memory_space=pltpu.VMEM)
+    hbm = pl.BlockSpec(memory_space=pltpu.HBM)
     dma = pltpu.SemaphoreType.DMA
     others = max(nh - 1, 1)
+    outputs = 2 * tokens * (width + state) * 4
+    limit = VMEM_BYTES - outputs - 2**16
     return pl.pallas_call(
         functools.partial(kernel, n, nh),
         out_shape=(
-            jax.ShapeDtypeStruct((tokens, width), F32),
-            jax.ShapeDtypeStruct((tokens, width), F32),
-            jax.ShapeDtypeStruct((tokens, state), F32),
-            jax.ShapeDtypeStruct((tokens, state), F32),
+            pltpu.VMEM((tokens, width), F32),
+            pltpu.VMEM((tokens, width), F32),
+            pltpu.VMEM((tokens, state), F32),
+            pltpu.VMEM((tokens, state), F32),
         ),
-        in_specs=[vmem] * 7,
+        in_specs=[hbm] + [vmem] * 5 + [hbm],
         out_specs=(vmem,) * 4,
         scratch_shapes=[
+            pltpu.VMEM((tokens, width), F32),
+            pltpu.VMEM((tokens, width), F32),
             pltpu.VMEM((tokens, width), F32),
             pltpu.VMEM((tokens, width), F32),
             pltpu.VMEM((tokens, width), BF16),
@@ -315,12 +336,16 @@
             dma((chunks,)),
             dma((chunks,)),
             dma((chunks,)),
-            dma((others,)),
-            dma((others,)),
+            dma((others, 2)),
+            dma((others, 2)),
             dma((1,)),
             dma((1,)),
+            dma((width // COLS,)),
+            dma((width // COLS,)),
         ],
-        compiler_params=pltpu.CompilerParams(collective_id=0, has_side_effects=True),
+        compiler_params=pltpu.CompilerParams(
+            collective_id=0, has_side_effects=True, vmem_limit_bytes=limit
+        ),
         name="mixer",
     )(inputs, rates, decay_rate[None, :], skip[None, :], keys_b, keys_c, grad_out)
 

time: 63.2 us -> 57.9 us (0.916)
  the two profiles are of different devices: /device:TPU:9 before, /device:TPU:11 now
where the time goes in v3:
time: 57.9 us; the launch traced here: 57.7 us
  Pallas kernels  53.1 us (92%)
  local copies, waits for them, and re-layouts  3.95 us (7%)
  between operations  0.64 us (1%)
    pallas_call x1, Pallas kernels, body(): pl.pallas_call(functools.partial(kernel, n, nh), out_shape=(pltpu.VMEM((t...  53.1 us
    unnamed x4, local copies, waits for them, and re-layouts  3.95 us

profile of v3, /device:TPU:11, one launch (start us, length us, event | category | flops | bytes accessed | tf_op | source)
XLA Modules:
  0.0 57.7 jit_solution(3658375166226721955)
XLA Ops:
  0.6 53.1 %mixer.1 = (f32[256,2048]{1,0:T(8,128)S(1)}, f32[256,2048]{1,0:T(8,128)S(1)}, f32[256,128]{1,0:T(8,128)S(1)}, f32[256,128]{1,0:T(8,128)S(1)}) custom-call(f32[256,2048]{1,0:T(8,128)} %x_hbm.1, f32[32,256]{1,0:T(8,128)} %rates_ref.1, f32[1,32]{1,0:T(1,128)} %bitcast.2, f32[1,32]{1,0:T(1,128)} %bitcast.3, f32[256,128]{1,0:T(8,128)} %b_ref.1, ...), custom_call_target="tpu_custom_call" | custom-call | tf_op jit(solution)/shard_map/mixer/pallas_call | solution.py:300
  53.8 1.3 %copy.15 = f32[256,2048]{1,0:T(8,128)} copy(f32[256,2048]{1,0:T(8,128)S(1)} %get-tuple-element.4) | data formatting | bytes 4194304
  55.1 0.7 %copy.17 = f32[256,128]{1,0:T(8,128)} copy(f32[256,128]{1,0:T(8,128)S(1)} %get-tuple-element.6) | data formatting | bytes 262144
  55.8 0.7 %copy.18 = f32[256,128]{1,0:T(8,128)} copy(f32[256,128]{1,0:T(8,128)S(1)} %get-tuple-element.7) | data formatting | bytes 262144
  56.4 1.3 %copy.16 = f32[256,2048]{1,0:T(8,128)} copy(f32[256,2048]{1,0:T(8,128)S(1)} %get-tuple-element.5) | data formatting | bytes 4194304
